TPU v7x, 32 devices: a whole 2x2x4 slice. The times are simulated.
32 devices in a mesh: parts: 2 (over y), section: 4 (over x, core), tile: 4 (over z).
Axes of the slice: x: 2, y: 2, z: 4, core: 2. Of those that a mesh axis runs over, the one named last changes fastest.
Arguments:
- frames: bfloat16 [8, 4, 16, 16, 128], P('parts', 'tile'), parts along dimension 0, may hold values from -8 to 8
- cache: bfloat16 [4, 4, 4, 16, 16, 128], P('section', 'parts', 'tile'), parts along dimension 1, may hold values from -4 to 4
- conv_weight: bfloat16 [4, 3, 3, 3, 128, 128], P('section'), may hold values from -0.109375 to 0.109375
- conv_bias: float32 [4, 128], P('section'), may hold values from -2 to 2
- norm_gain: float32 [4, 128], P('section'), may hold values from 0.1 to 1.9
- norm_bias: float32 [4, 128], P('section'), may hold values from -2 to 2
Outputs:
- section_outputs: bfloat16 [4, 8, 4, 16, 16, 128], P('section', 'parts', 'tile'), parts along dimension 1
There are 2 independent parts, one for each index of `parts`. A program takes and returns all parts, laid end to end along the dimension named above; an argument that names none is the same for every part. Nothing has to cross between parts.
All inputs are finite; a program needn't handle non-finite values.
Results may differ from a plain program's by a relative error of at most 0.0056.
Values may be sent and summed in bfloat16 or wider, within the bound.
A program may use at most 64 MiB of HBM per device.

v0:
```python
import jax
import jax.numpy as jnp
from jax import lax
from jax.sharding import PartitionSpec as P

GROUPS = 32


EPSILON = 1e-06


def from_behind(array, axis, by):
    peers = lax.axis_size(axis)
    return lax.ppermute(array, axis, [(i, (i + by) % peers) for i in range(peers)])


def passed_along(value, axis, steps):
    count = lax.axis_size(axis)
    first, last = (max(0, -steps), min(count, count - steps))
    return lax.ppermute(value, axis, [(source, source + steps) for source in range(first, last)])


def normalize(inputs, gain, offset):
    count, height, width, channels = inputs.shape
    values = inputs.astype(jnp.float32).reshape(count, height * width, GROUPS, channels // GROUPS)
    members = height * width * (channels // GROUPS) * lax.axis_size("tile")
    total, squares = lax.psum(
        (jnp.sum(values, axis=(1, 3)), jnp.sum(values * values, axis=(1, 3))), "tile"
    )
    mean = (total / members)[:, None, :, None]
    variance = jnp.maximum((squares / members)[:, None, :, None] - mean * mean, 0.0)
    centered = values - mean
    normed = (centered / jnp.sqrt(variance + EPSILON)).reshape(inputs.shape)
    return jax.nn.silu(normed * gain + offset).astype(jnp.bfloat16)


def extend(active):
    tiles = lax.axis_size("tile")
    across = min(8, tiles // 2)
    rows_all = tiles // across
    placed = (lax.axis_index("tile") + across + 2) % tiles
    column = placed % across
    row_at = placed // across
    nothing = jnp.zeros((), active.dtype)
    left = from_behind(active[:, :, -1:], "tile", 1)
    left = jnp.where(column == 0, nothing, left)
    right = from_behind(active[:, :, :1], "tile", -1)
    right = jnp.where(column == across - 1, nothing, right)
    wide = jnp.concatenate([left, active, right], axis=2)
    above = from_behind(wide[:, -1:], "tile", across)
    above = jnp.where(row_at == 0, nothing, above)
    below = from_behind(wide[:, :1], "tile", -across)
    below = jnp.where(row_at == rows_all - 1, nothing, below)
    return jnp.concatenate([above, wide, below], axis=1)


def convolve(padded, kernel, count):
    height = padded.shape[1] - 2
    width = padded.shape[2] - 2
    channels = padded.shape[3]
    pieces = [
        padded[step_t : step_t + count, step_y : step_y + height, step_x : step_x + width]
        for step_t in range(3)
        for step_y in range(3)
        for step_x in range(3)
    ]
    patches = jnp.concatenate(pieces, axis=3).reshape(count * height * width, 27 * channels)
    result = jnp.dot(
        patches, kernel.reshape(27 * channels, channels), preferred_element_type=jnp.float32
    )
    return result.reshape(count, height, width, channels)


def local(frames, cache, conv_weight, conv_bias, norm_gain, norm_bias):
    kernel = conv_weight[0]
    bias = conv_bias[0]
    gain = norm_gain[0]
    offset = norm_bias[0]
    sections = lax.axis_size("section")
    position = lax.axis_index("section")
    inputs = frames[:, 0]
    history = extend(cache[0, :, 0])
    count = inputs.shape[0]
    result = jnp.zeros_like(inputs)
    current = inputs
    for tick in range(sections):
        active = normalize(current, gain, offset)
        padded = jnp.concatenate([history, extend(active)], axis=0)
        output = (current.astype(jnp.float32) + convolve(padded, kernel, count) + bias).astype(
            jnp.bfloat16
        )
        result = jnp.where(position == tick, output, result)
        if tick + 1 < sections:
            current = passed_along(output, "section", 1)
    return result[None, :, None]


def solution(mesh):
    placed = (
        P("parts", "tile", None, None, None),
        P("section", "parts", "tile", None, None, None),
        P("section", None, None, None, None, None),
        P("section", None),
        P("section", None),
        P("section", None),
    )
    return jax.shard_map(
        local,
        mesh=mesh,
        in_specs=placed,
        out_specs=P("section", "parts", "tile", None, None, None),
        check_vma=False,
    )
```

profile of v0, /device:TPU:6, one launch (start us, length us, event | category | flops | bytes accessed | tf_op | source)
XLA Modules:
  0.0 150.2 jit_solution(14677981788090294342)
XLA Ops:
  1.0 3.7 %collective-permute-start.1 = (bf16[2,16,1,128]{3,2,1,0:T(2,128)(2,1)S(1)}, bf16[2,16,1,128]{3,2,1,0:T(2,128)(2,1)S(1)}, u32[]{:S(2)}, u32[]{:S(2)}) collective-permute-start(bf16[2,16,1,128]{3,2,1,0:T(2,128)(2,1)S(1)} %get-tuple-element.48), channel_id=1, source_target_pairs={{0,3},{1,0},{2,1},{3,2},{4,7},{5,4},{6,5},{7,6},{8,11},{9,8},{10,9... | collective-permute-start | bytes 24584 | tf_op jit(solution)/shard_map/ppermute | solution.py:14
  6.1 8.8 %all-reduce.3 = (f32[4,32]{1,0:T(4,128)S(1)}, f32[4,32]{1,0:T(4,128)S(1)}) all-reduce(f32[4,32]{1,0:T(4,128)S(1)} %reduce_sum.100, f32[4,32]{1,0:T(4,128)S(1)} %reduce_sum.97), channel_id=1, replica_groups=mesh['parts'=2,'section'=4,'tile'=4] {'tile'}, use_global_device_ids=true, to_apply=%region_5.6 | all-reduce | flops 256 | bytes 2048 | tf_op jit(solution)/shard_map/psum | solution.py:27
  20.2 4.0 %collective-permute-done = bf16[2,16,1,128]{3,2,1,0:T(2,128)(2,1)S(1)} collective-permute-done((bf16[2,16,1,128]{3,2,1,0:T(2,128)(2,1)S(1)}, bf16[2,16,1,128]{3,2,1,0:T(2,128)(2,1)S(1)}, u32[]{:S(2)}, u32[]{:S(2)}) %collective-permute-start) | collective-permute-done | bytes 8224 | tf_op jit(solution)/shard_map/ppermute | solution.py:14
  25.0 2.9 %collective-permute-start.2 = (bf16[2,1,18,128]{3,2,1,0:T(8,128)(2,1)S(1)}, bf16[2,1,18,128]{3,2,1,0:T(8,128)(2,1)S(1)}, u32[]{:S(2)}, u32[]{:S(2)}) collective-permute-start(bf16[2,1,18,128]{3,2,1,0:T(8,128)(2,1)S(1)} %get-tuple-element.45), channel_id=1, source_target_pairs={{0,2},{1,3},{2,0},{3,1},{4,6},{5,7},{6,4},{7,5},{8,10},{9,11},{10,... | collective-permute-start | bytes 27656 | tf_op jit(solution)/shard_map/ppermute | solution.py:14
  28.2 2.8 %collective-permute-start.6 = (bf16[4,1,18,128]{3,2,1,0:T(8,128)(2,1)S(1)}, bf16[4,1,18,128]{3,2,1,0:T(8,128)(2,1)S(1)}, u32[]{:S(2)}, u32[]{:S(2)}) collective-permute-start(bf16[4,1,18,128]{3,2,1,0:T(8,128)(2,1)S(1)} %get-tuple-element.35), channel_id=1, source_target_pairs={{0,2},{1,3},{2,0},{3,1},{4,6},{5,7},{6,4},{7,5},{8,10},{9,11},{10,... | collective-permute-start | bytes 55304 | tf_op jit(solution)/shard_map/ppermute | solution.py:14
  38.0 2.0 %fusion.7 = bf16[4,16,16,128]{3,2,1,0:T(8,128)(2,1)S(1)} fusion(bf16[4,16,16,3456]{3,2,1,0:T(8,128)(2,1)S(1)} %slice_dynamic-update-slice_fusion.72, bf16[3456,128,1,1]{1,0,3,2:T(8,128)(2,1)S(1)} %bitcast.44, bf16[4,1,16,16,128]{4,3,2,1,0:T(8,128)(2,1)S(1)} %copy-done.2, f32[128]{0:T(128)S(1)} %bitcast.70), kind=kOutput, calls=%fused_computation.11 | convolution fusion | flops 906493952 | bytes 8487424 | tf_op jit(solution)/shard_map/dot_general | solution.py:68
  40.0 1.9 %collective-permute-start.8 = (bf16[4,16,16,128]{3,2,1,0:T(8,128)(2,1)S(1)}, bf16[4,16,16,128]{3,2,1,0:T(8,128)(2,1)S(1)}, u32[]{:S(2)}, u32[]{:S(2)}) collective-permute-start(bf16[4,16,16,128]{3,2,1,0:T(8,128)(2,1)S(1)} %fusion.7), channel_id=1, source_target_pairs={{0,4},{4,8},{8,12},{1,5},{5,9},{9,13},{2,6},{6,10},{10,14},{3,7},{... | collective-permute-start | bytes 786440 | tf_op jit(solution)/shard_map/ppermute | solution.py:20
  41.9 5.8 %collective-permute-done.8 = bf16[4,16,16,128]{3,2,1,0:T(8,128)(2,1)S(1)} collective-permute-done((bf16[4,16,16,128]{3,2,1,0:T(8,128)(2,1)S(1)}, bf16[4,16,16,128]{3,2,1,0:T(8,128)(2,1)S(1)}, u32[]{:S(2)}, u32[]{:S(2)}) %collective-permute-start.8) | collective-permute-done | bytes 262176 | tf_op jit(solution)/shard_map/ppermute | solution.py:20
  48.2 10.2 %all-reduce.2 = (f32[4,32]{1,0:T(4,128)S(1)}, f32[4,32]{1,0:T(4,128)S(1)}) all-reduce(f32[4,32]{1,0:T(4,128)S(1)} %reduce_sum.112, f32[4,32]{1,0:T(4,128)S(1)} %reduce_sum.106), channel_id=1, replica_groups=mesh['parts'=2,'section'=4,'tile'=4] {'tile'}, use_global_device_ids=true, to_apply=%region_11.12 | all-reduce | flops 256 | bytes 2048 | tf_op jit(solution)/shard_map/psum | solution.py:27
  63.1 2.2 %collective-permute-done.9 = bf16[4,16,1,128]{3,2,1,0:T(2,128)(2,1)S(1)} collective-permute-done((bf16[4,16,1,128]{3,2,1,0:T(2,128)(2,1)S(1)}, bf16[4,16,1,128]{3,2,1,0:T(2,128)(2,1)S(1)}, u32[]{:S(2)}, u32[]{:S(2)}) %collective-permute-start.9) | collective-permute-done | bytes 16416 | tf_op jit(solution)/shard_map/ppermute | solution.py:14
  65.5 2.9 %collective-permute-start.11 = (bf16[4,1,18,128]{3,2,1,0:T(8,128)(2,1)S(1)}, bf16[4,1,18,128]{3,2,1,0:T(8,128)(2,1)S(1)}, u32[]{:S(2)}, u32[]{:S(2)}) collective-permute-start(bf16[4,1,18,128]{3,2,1,0:T(8,128)(2,1)S(1)} %get-tuple-element.31), channel_id=1, source_target_pairs={{0,2},{1,3},{2,0},{3,1},{4,6},{5,7},{6,4},{7,5},{8,10},{9,11},{10,... | collective-permute-start | bytes 55304 | tf_op jit(solution)/shard_map/ppermute | solution.py:14
  74.6 2.0 %fusion.6 = bf16[4,16,16,128]{3,2,1,0:T(8,128)(2,1)S(1)} fusion(bf16[4,16,16,3456]{3,2,1,0:T(8,128)(2,1)S(1)} %slice_dynamic-update-slice_fusion.48, bf16[3456,128,1,1]{1,0,3,2:T(8,128)(2,1)S(1)} %bitcast.45, bf16[4,16,16,128]{3,2,1,0:T(8,128)(2,1)S(1)} %collective-permute-done.8, f32[128]{0:T(128)S(1)} %bitcast.71), kind=kOutput, calls=%fused_computation.10 | convolution fusion | flops 906493952 | bytes 8487424 | tf_op jit(solution)/shard_map/dot_general | solution.py:68
  76.6 1.9 %collective-permute-start.13 = (bf16[4,16,16,128]{3,2,1,0:T(8,128)(2,1)S(1)}, bf16[4,16,16,128]{3,2,1,0:T(8,128)(2,1)S(1)}, u32[]{:S(2)}, u32[]{:S(2)}) collective-permute-start(bf16[4,16,16,128]{3,2,1,0:T(8,128)(2,1)S(1)} %fusion.6), channel_id=1, source_target_pairs={{0,4},{4,8},{8,12},{1,5},{5,9},{9,13},{2,6},{6,10},{10,14},{3,7},{... | collective-permute-start | bytes 786440 | tf_op jit(solution)/shard_map/ppermute | solution.py:20
  78.5 5.8 %collective-permute-done.13 = bf16[4,16,16,128]{3,2,1,0:T(8,128)(2,1)S(1)} collective-permute-done((bf16[4,16,16,128]{3,2,1,0:T(8,128)(2,1)S(1)}, bf16[4,16,16,128]{3,2,1,0:T(8,128)(2,1)S(1)}, u32[]{:S(2)}, u32[]{:S(2)}) %collective-permute-start.13) | collective-permute-done | bytes 262176 | tf_op jit(solution)/shard_map/ppermute | solution.py:20
  84.8 10.0 %all-reduce.1 = (f32[4,32]{1,0:T(4,128)S(1)}, f32[4,32]{1,0:T(4,128)S(1)}) all-reduce(f32[4,32]{1,0:T(4,128)S(1)} %reduce_sum.145, f32[4,32]{1,0:T(4,128)S(1)} %reduce_sum.115), channel_id=1, replica_groups=mesh['parts'=2,'section'=4,'tile'=4] {'tile'}, use_global_device_ids=true, to_apply=%region_17.18 | all-reduce | flops 256 | bytes 2048 | tf_op jit(solution)/shard_map/psum | solution.py:27
  99.5 2.2 %collective-permute-done.14 = bf16[4,16,1,128]{3,2,1,0:T(2,128)(2,1)S(1)} collective-permute-done((bf16[4,16,1,128]{3,2,1,0:T(2,128)(2,1)S(1)}, bf16[4,16,1,128]{3,2,1,0:T(2,128)(2,1)S(1)}, u32[]{:S(2)}, u32[]{:S(2)}) %collective-permute-start.14) | collective-permute-done | bytes 16416 | tf_op jit(solution)/shard_map/ppermute | solution.py:14
  101.9 2.9 %collective-permute-start.16 = (bf16[4,1,18,128]{3,2,1,0:T(8,128)(2,1)S(1)}, bf16[4,1,18,128]{3,2,1,0:T(8,128)(2,1)S(1)}, u32[]{:S(2)}, u32[]{:S(2)}) collective-permute-start(bf16[4,1,18,128]{3,2,1,0:T(8,128)(2,1)S(1)} %get-tuple-element.27), channel_id=1, source_target_pairs={{0,2},{1,3},{2,0},{3,1},{4,6},{5,7},{6,4},{7,5},{8,10},{9,11},{10,... | collective-permute-start | bytes 55304 | tf_op jit(solution)/shard_map/ppermute | solution.py:14
  111.0 2.0 %fusion.5 = bf16[4,16,16,128]{3,2,1,0:T(8,128)(2,1)S(1)} fusion(bf16[4,16,16,3456]{3,2,1,0:T(8,128)(2,1)S(1)} %slice_dynamic-update-slice_fusion.24, bf16[3456,128,1,1]{1,0,3,2:T(8,128)(2,1)S(1)} %bitcast.46, bf16[4,16,16,128]{3,2,1,0:T(8,128)(2,1)S(1)} %collective-permute-done.13, f32[128]{0:T(128)S(1)} %bitcast.72), kind=kOutput, calls=%fused_computation.9 | convolution fusion | flops 906493952 | bytes 8487424 | tf_op jit(solution)/shard_map/dot_general | solution.py:68
  114.9 5.8 %collective-permute-done.18 = bf16[4,16,16,128]{3,2,1,0:T(8,128)(2,1)S(1)} collective-permute-done((bf16[4,16,16,128]{3,2,1,0:T(8,128)(2,1)S(1)}, bf16[4,16,16,128]{3,2,1,0:T(8,128)(2,1)S(1)}, u32[]{:S(2)}, u32[]{:S(2)}) %collective-permute-start.18) | collective-permute-done | bytes 262176 | tf_op jit(solution)/shard_map/ppermute | solution.py:20
  121.2 10.2 %all-reduce = (f32[4,32]{1,0:T(4,128)S(1)}, f32[4,32]{1,0:T(4,128)S(1)}) all-reduce(f32[4,32]{1,0:T(4,128)S(1)} %reduce_sum.151, f32[4,32]{1,0:T(4,128)S(1)} %reduce_sum.148), channel_id=1, replica_groups=mesh['parts'=2,'section'=4,'tile'=4] {'tile'}, use_global_device_ids=true, to_apply=%region_23.24 | all-reduce | flops 256 | bytes 2048 | tf_op jit(solution)/shard_map/psum | solution.py:27
  136.1 2.2 %collective-permute-done.19 = bf16[4,16,1,128]{3,2,1,0:T(2,128)(2,1)S(1)} collective-permute-done((bf16[4,16,1,128]{3,2,1,0:T(2,128)(2,1)S(1)}, bf16[4,16,1,128]{3,2,1,0:T(2,128)(2,1)S(1)}, u32[]{:S(2)}, u32[]{:S(2)}) %collective-permute-start.19) | collective-permute-done | bytes 16416 | tf_op jit(solution)/shard_map/ppermute | solution.py:14
  138.4 2.9 %collective-permute-start.21 = (bf16[4,1,18,128]{3,2,1,0:T(8,128)(2,1)S(1)}, bf16[4,1,18,128]{3,2,1,0:T(8,128)(2,1)S(1)}, u32[]{:S(2)}, u32[]{:S(2)}) collective-permute-start(bf16[4,1,18,128]{3,2,1,0:T(8,128)(2,1)S(1)} %get-tuple-element.23), channel_id=1, source_target_pairs={{0,2},{1,3},{2,0},{3,1},{4,6},{5,7},{6,4},{7,5},{8,10},{9,11},{10,... | collective-permute-start | bytes 55304 | tf_op jit(solution)/shard_map/ppermute | solution.py:14
  141.3 2.1 %collective-permute-done.22 = bf16[4,1,18,128]{3,2,1,0:T(8,128)(2,1)S(1)} collective-permute-done((bf16[4,1,18,128]{3,2,1,0:T(8,128)(2,1)S(1)}, bf16[4,1,18,128]{3,2,1,0:T(8,128)(2,1)S(1)}, u32[]{:S(2)}, u32[]{:S(2)}) %collective-permute-start.22) | collective-permute-done | bytes 18464 | tf_op jit(solution)/shard_map/ppermute | solution.py:14
  147.5 2.7 %fusion.9 = bf16[1,4,1,16,16,128]{5,4,3,2,1,0:T(8,128)(2,1)} fusion(bf16[4,16,16,3456]{3,2,1,0:T(8,128)(2,1)S(1)} %slice_dynamic-update-slice_fusion, bf16[3456,128,1,1]{1,0,3,2:T(8,128)(2,1)S(1)} %bitcast.47, bf16[4,16,16,128]{3,2,1,0:T(8,128)(2,1)S(1)} %collective-permute-done.18, bf16[4,16,16,128]{3,2,1,0:T(8,128)(2,1)S(1)} %fusion.5, ...), kind=kOutput, calls=%fused_computation.13 | convolution fusion | flops 907018240 | bytes 9273860 | tf_op jit(solution)/shard_map/dot_general | solution.py:68
  (232 shorter events, 49.2 us)
Async XLA Ops:
  0.0 38.0 %copy-start = (bf16[1,3,3,3,128,128]{5,4,3,2,1,0:T(8,128)(2,1)S(1)}, bf16[1,3,3,3,128,128]{5,4,3,2,1,0:T(8,128)(2,1)}, u32[]{:S(2)}) copy-start(bf16[1,3,3,3,128,128]{5,4,3,2,1,0:T(8,128)(2,1)} %param.8) | copy-start | bytes 2654212
  1.0 19.2 %collective-permute-start.1 = (bf16[2,16,1,128]{3,2,1,0:T(2,128)(2,1)S(1)}, bf16[2,16,1,128]{3,2,1,0:T(2,128)(2,1)S(1)}, u32[]{:S(2)}, u32[]{:S(2)}) collective-permute-start(bf16[2,16,1,128]{3,2,1,0:T(2,128)(2,1)S(1)} %get-tuple-element.48), channel_id=1, source_target_pairs={{0,3},{1,0},{2,1},{3,2},{4,7},{5,4},{6,5},{7,6},{8,11},{9,8},{10,9... | collective-permute-start | bytes 24584 | tf_op jit(solution)/shard_map/ppermute | solution.py:14
  16.6 11.4 %collective-permute-start.5 = (bf16[4,16,1,128]{3,2,1,0:T(2,128)(2,1)S(1)}, bf16[4,16,1,128]{3,2,1,0:T(2,128)(2,1)S(1)}, u32[]{:S(2)}, u32[]{:S(2)}) collective-permute-start(bf16[4,16,1,128]{3,2,1,0:T(2,128)(2,1)S(1)} %get-tuple-element.44), channel_id=1, source_target_pairs={{0,3},{1,0},{2,1},{3,2},{4,7},{5,4},{6,5},{7,6},{8,11},{9,8},{10,9... | collective-permute-start | bytes 49160 | tf_op jit(solution)/shard_map/ppermute | solution.py:14
  18.2 9.8 %collective-permute-start.4 = (bf16[4,16,1,128]{3,2,1,0:T(2,128)(2,1)S(1)}, bf16[4,16,1,128]{3,2,1,0:T(2,128)(2,1)S(1)}, u32[]{:S(2)}, u32[]{:S(2)}) collective-permute-start(bf16[4,16,1,128]{3,2,1,0:T(2,128)(2,1)S(1)} %get-tuple-element.43), channel_id=1, source_target_pairs={{0,1},{1,2},{2,3},{3,0},{4,5},{5,6},{6,7},{7,4},{8,9},{9,10},{10,1... | collective-permute-start | bytes 49160 | tf_op jit(solution)/shard_map/ppermute | solution.py:14
  18.6 5.5 %collective-permute-start = (bf16[2,16,1,128]{3,2,1,0:T(2,128)(2,1)S(1)}, bf16[2,16,1,128]{3,2,1,0:T(2,128)(2,1)S(1)}, u32[]{:S(2)}, u32[]{:S(2)}) collective-permute-start(bf16[2,16,1,128]{3,2,1,0:T(2,128)(2,1)S(1)} %get-tuple-element.47), channel_id=1, source_target_pairs={{0,1},{1,2},{2,3},{3,0},{4,5},{5,6},{6,7},{7,4},{8,9},{9,10},{10,1... | collective-permute-start | bytes 24584 | tf_op jit(solution)/shard_map/ppermute | solution.py:14
  24.9 6.1 %collective-permute-start.3 = (bf16[2,1,18,128]{3,2,1,0:T(8,128)(2,1)S(1)}, bf16[2,1,18,128]{3,2,1,0:T(8,128)(2,1)S(1)}, u32[]{:S(2)}, u32[]{:S(2)}) collective-permute-start(bf16[2,1,18,128]{3,2,1,0:T(8,128)(2,1)S(1)} %get-tuple-element.46), channel_id=1, source_target_pairs={{0,2},{1,3},{2,0},{3,1},{4,6},{5,7},{6,4},{7,5},{8,10},{9,11},{10,... | collective-permute-start | bytes 27656 | tf_op jit(solution)/shard_map/ppermute | solution.py:14
  25.0 6.1 %collective-permute-start.2 = (bf16[2,1,18,128]{3,2,1,0:T(8,128)(2,1)S(1)}, bf16[2,1,18,128]{3,2,1,0:T(8,128)(2,1)S(1)}, u32[]{:S(2)}, u32[]{:S(2)}) collective-permute-start(bf16[2,1,18,128]{3,2,1,0:T(8,128)(2,1)S(1)} %get-tuple-element.45), channel_id=1, source_target_pairs={{0,2},{1,3},{2,0},{3,1},{4,6},{5,7},{6,4},{7,5},{8,10},{9,11},{10,... | collective-permute-start | bytes 27656 | tf_op jit(solution)/shard_map/ppermute | solution.py:14
  28.1 4.8 %collective-permute-start.7 = (bf16[4,1,18,128]{3,2,1,0:T(8,128)(2,1)S(1)}, bf16[4,1,18,128]{3,2,1,0:T(8,128)(2,1)S(1)}, u32[]{:S(2)}, u32[]{:S(2)}) collective-permute-start(bf16[4,1,18,128]{3,2,1,0:T(8,128)(2,1)S(1)} %get-tuple-element.36), channel_id=1, source_target_pairs={{0,2},{1,3},{2,0},{3,1},{4,6},{5,7},{6,4},{7,5},{8,10},{9,11},{10,... | collective-permute-start | bytes 55304 | tf_op jit(solution)/shard_map/ppermute | solution.py:14
  28.2 4.9 %collective-permute-start.6 = (bf16[4,1,18,128]{3,2,1,0:T(8,128)(2,1)S(1)}, bf16[4,1,18,128]{3,2,1,0:T(8,128)(2,1)S(1)}, u32[]{:S(2)}, u32[]{:S(2)}) collective-permute-start(bf16[4,1,18,128]{3,2,1,0:T(8,128)(2,1)S(1)} %get-tuple-element.35), channel_id=1, source_target_pairs={{0,2},{1,3},{2,0},{3,1},{4,6},{5,7},{6,4},{7,5},{8,10},{9,11},{10,... | collective-permute-start | bytes 55304 | tf_op jit(solution)/shard_map/ppermute | solution.py:14
  40.0 7.7 %collective-permute-start.8 = (bf16[4,16,16,128]{3,2,1,0:T(8,128)(2,1)S(1)}, bf16[4,16,16,128]{3,2,1,0:T(8,128)(2,1)S(1)}, u32[]{:S(2)}, u32[]{:S(2)}) collective-permute-start(bf16[4,16,16,128]{3,2,1,0:T(8,128)(2,1)S(1)} %fusion.7), channel_id=1, source_target_pairs={{0,4},{4,8},{8,12},{1,5},{5,9},{9,13},{2,6},{6,10},{10,14},{3,7},{... | collective-permute-start | bytes 786440 | tf_op jit(solution)/shard_map/ppermute | solution.py:20
  59.1 4.0 %collective-permute-start.10 = (bf16[4,16,1,128]{3,2,1,0:T(2,128)(2,1)S(1)}, bf16[4,16,1,128]{3,2,1,0:T(2,128)(2,1)S(1)}, u32[]{:S(2)}, u32[]{:S(2)}) collective-permute-start(bf16[4,16,1,128]{3,2,1,0:T(2,128)(2,1)S(1)} %get-tuple-element.42), channel_id=1, source_target_pairs={{0,3},{1,0},{2,1},{3,2},{4,7},{5,4},{6,5},{7,6},{8,11},{9,8},{10,9... | collective-permute-start | bytes 49160 | tf_op jit(solution)/shard_map/ppermute | solution.py:14
  59.6 5.7 %collective-permute-start.9 = (bf16[4,16,1,128]{3,2,1,0:T(2,128)(2,1)S(1)}, bf16[4,16,1,128]{3,2,1,0:T(2,128)(2,1)S(1)}, u32[]{:S(2)}, u32[]{:S(2)}) collective-permute-start(bf16[4,16,1,128]{3,2,1,0:T(2,128)(2,1)S(1)} %get-tuple-element.41), channel_id=1, source_target_pairs={{0,1},{1,2},{2,3},{3,0},{4,5},{5,6},{6,7},{7,4},{8,9},{9,10},{10,1... | collective-permute-start | bytes 49160 | tf_op jit(solution)/shard_map/ppermute | solution.py:14
  65.4 4.8 %collective-permute-start.12 = (bf16[4,1,18,128]{3,2,1,0:T(8,128)(2,1)S(1)}, bf16[4,1,18,128]{3,2,1,0:T(8,128)(2,1)S(1)}, u32[]{:S(2)}, u32[]{:S(2)}) collective-permute-start(bf16[4,1,18,128]{3,2,1,0:T(8,128)(2,1)S(1)} %get-tuple-element.32), channel_id=1, source_target_pairs={{0,2},{1,3},{2,0},{3,1},{4,6},{5,7},{6,4},{7,5},{8,10},{9,11},{10,... | collective-permute-start | bytes 55304 | tf_op jit(solution)/shard_map/ppermute | solution.py:14
  65.5 5.2 %collective-permute-start.11 = (bf16[4,1,18,128]{3,2,1,0:T(8,128)(2,1)S(1)}, bf16[4,1,18,128]{3,2,1,0:T(8,128)(2,1)S(1)}, u32[]{:S(2)}, u32[]{:S(2)}) collective-permute-start(bf16[4,1,18,128]{3,2,1,0:T(8,128)(2,1)S(1)} %get-tuple-element.31), channel_id=1, source_target_pairs={{0,2},{1,3},{2,0},{3,1},{4,6},{5,7},{6,4},{7,5},{8,10},{9,11},{10,... | collective-permute-start | bytes 55304 | tf_op jit(solution)/shard_map/ppermute | solution.py:14
  76.6 7.7 %collective-permute-start.13 = (bf16[4,16,16,128]{3,2,1,0:T(8,128)(2,1)S(1)}, bf16[4,16,16,128]{3,2,1,0:T(8,128)(2,1)S(1)}, u32[]{:S(2)}, u32[]{:S(2)}) collective-permute-start(bf16[4,16,16,128]{3,2,1,0:T(8,128)(2,1)S(1)} %fusion.6), channel_id=1, source_target_pairs={{0,4},{4,8},{8,12},{1,5},{5,9},{9,13},{2,6},{6,10},{10,14},{3,7},{... | collective-permute-start | bytes 786440 | tf_op jit(solution)/shard_map/ppermute | solution.py:20
  95.5 4.0 %collective-permute-start.15 = (bf16[4,16,1,128]{3,2,1,0:T(2,128)(2,1)S(1)}, bf16[4,16,1,128]{3,2,1,0:T(2,128)(2,1)S(1)}, u32[]{:S(2)}, u32[]{:S(2)}) collective-permute-start(bf16[4,16,1,128]{3,2,1,0:T(2,128)(2,1)S(1)} %get-tuple-element.40), channel_id=1, source_target_pairs={{0,3},{1,0},{2,1},{3,2},{4,7},{5,4},{6,5},{7,6},{8,11},{9,8},{10,9... | collective-permute-start | bytes 49160 | tf_op jit(solution)/shard_map/ppermute | solution.py:14
  96.0 5.7 %collective-permute-start.14 = (bf16[4,16,1,128]{3,2,1,0:T(2,128)(2,1)S(1)}, bf16[4,16,1,128]{3,2,1,0:T(2,128)(2,1)S(1)}, u32[]{:S(2)}, u32[]{:S(2)}) collective-permute-start(bf16[4,16,1,128]{3,2,1,0:T(2,128)(2,1)S(1)} %get-tuple-element.39), channel_id=1, source_target_pairs={{0,1},{1,2},{2,3},{3,0},{4,5},{5,6},{6,7},{7,4},{8,9},{9,10},{10,1... | collective-permute-start | bytes 49160 | tf_op jit(solution)/shard_map/ppermute | solution.py:14
  101.8 4.8 %collective-permute-start.17 = (bf16[4,1,18,128]{3,2,1,0:T(8,128)(2,1)S(1)}, bf16[4,1,18,128]{3,2,1,0:T(8,128)(2,1)S(1)}, u32[]{:S(2)}, u32[]{:S(2)}) collective-permute-start(bf16[4,1,18,128]{3,2,1,0:T(8,128)(2,1)S(1)} %get-tuple-element.28), channel_id=1, source_target_pairs={{0,2},{1,3},{2,0},{3,1},{4,6},{5,7},{6,4},{7,5},{8,10},{9,11},{10,... | collective-permute-start | bytes 55304 | tf_op jit(solution)/shard_map/ppermute | solution.py:14
  101.9 5.2 %collective-permute-start.16 = (bf16[4,1,18,128]{3,2,1,0:T(8,128)(2,1)S(1)}, bf16[4,1,18,128]{3,2,1,0:T(8,128)(2,1)S(1)}, u32[]{:S(2)}, u32[]{:S(2)}) collective-permute-start(bf16[4,1,18,128]{3,2,1,0:T(8,128)(2,1)S(1)} %get-tuple-element.27), channel_id=1, source_target_pairs={{0,2},{1,3},{2,0},{3,1},{4,6},{5,7},{6,4},{7,5},{8,10},{9,11},{10,... | collective-permute-start | bytes 55304 | tf_op jit(solution)/shard_map/ppermute | solution.py:14
  113.0 7.7 %collective-permute-start.18 = (bf16[4,16,16,128]{3,2,1,0:T(8,128)(2,1)S(1)}, bf16[4,16,16,128]{3,2,1,0:T(8,128)(2,1)S(1)}, u32[]{:S(2)}, u32[]{:S(2)}) collective-permute-start(bf16[4,16,16,128]{3,2,1,0:T(8,128)(2,1)S(1)} %fusion.5), channel_id=1, source_target_pairs={{0,4},{4,8},{8,12},{1,5},{5,9},{9,13},{2,6},{6,10},{10,14},{3,7},{... | collective-permute-start | bytes 786440 | tf_op jit(solution)/shard_map/ppermute | solution.py:20
  132.0 4.0 %collective-permute-start.20 = (bf16[4,16,1,128]{3,2,1,0:T(2,128)(2,1)S(1)}, bf16[4,16,1,128]{3,2,1,0:T(2,128)(2,1)S(1)}, u32[]{:S(2)}, u32[]{:S(2)}) collective-permute-start(bf16[4,16,1,128]{3,2,1,0:T(2,128)(2,1)S(1)} %get-tuple-element.38), channel_id=1, source_target_pairs={{0,3},{1,0},{2,1},{3,2},{4,7},{5,4},{6,5},{7,6},{8,11},{9,8},{10,9... | collective-permute-start | bytes 49160 | tf_op jit(solution)/shard_map/ppermute | solution.py:14
  132.6 5.7 %collective-permute-start.19 = (bf16[4,16,1,128]{3,2,1,0:T(2,128)(2,1)S(1)}, bf16[4,16,1,128]{3,2,1,0:T(2,128)(2,1)S(1)}, u32[]{:S(2)}, u32[]{:S(2)}) collective-permute-start(bf16[4,16,1,128]{3,2,1,0:T(2,128)(2,1)S(1)} %get-tuple-element.37), channel_id=1, source_target_pairs={{0,1},{1,2},{2,3},{3,0},{4,5},{5,6},{6,7},{7,4},{8,9},{9,10},{10,1... | collective-permute-start | bytes 49160 | tf_op jit(solution)/shard_map/ppermute | solution.py:14
  138.3 5.1 %collective-permute-start.22 = (bf16[4,1,18,128]{3,2,1,0:T(8,128)(2,1)S(1)}, bf16[4,1,18,128]{3,2,1,0:T(8,128)(2,1)S(1)}, u32[]{:S(2)}, u32[]{:S(2)}) collective-permute-start(bf16[4,1,18,128]{3,2,1,0:T(8,128)(2,1)S(1)} %get-tuple-element.24), channel_id=1, source_target_pairs={{0,2},{1,3},{2,0},{3,1},{4,6},{5,7},{6,4},{7,5},{8,10},{9,11},{10,... | collective-permute-start | bytes 55304 | tf_op jit(solution)/shard_map/ppermute | solution.py:14
  138.4 5.2 %collective-permute-start.21 = (bf16[4,1,18,128]{3,2,1,0:T(8,128)(2,1)S(1)}, bf16[4,1,18,128]{3,2,1,0:T(8,128)(2,1)S(1)}, u32[]{:S(2)}, u32[]{:S(2)}) collective-permute-start(bf16[4,1,18,128]{3,2,1,0:T(8,128)(2,1)S(1)} %get-tuple-element.23), channel_id=1, source_target_pairs={{0,2},{1,3},{2,0},{3,1},{4,6},{5,7},{6,4},{7,5},{8,10},{9,11},{10,... | collective-permute-start | bytes 55304 | tf_op jit(solution)/shard_map/ppermute | solution.py:14
  (5 other events, 63.7 us)
where the time goes:
time: 151 us; the launch traced here: 150 us
  waiting for transfers between devices  42.6 us (28%)
  blocking collectives  39.2 us (26%)
  starting transfers between devices  34.2 us (23%)
  local copies, waits for them, and re-layouts  13.4 us (9%)
  other arithmetic  11 us (7%)
  matrix products  8.72 us (6%)
    psum x4, blocking collectives, normalize(): lax.psum((jnp.sum(values, axis=(1, 3)), jnp.sum(values * values, axis=(1,...  39.2 us
    ppermute x20, starting transfers between devices, from_behind(): lax.ppermute(array, axis, [(i, (i + by) % peers) for i in range(peers)])  28.4 us
    ppermute x20, waiting for transfers between devices, from_behind(): lax.ppermute(array, axis, [(i, (i + by) % peers) for i in range(peers)])  25.3 us
    ppermute x3, waiting for transfers between devices, passed_along(): lax.ppermute(value, axis, [(source, source + steps) for source in range(f...  17.3 us
    unnamed x104, local copies, waits for them, and re-layouts  9.31 us
    dot_general x4, matrix products, convolve(): jnp.dot(patches, kernel.reshape(27 * channels, channels), preferred_eleme...  8.72 us
    ppermute x3, starting transfers between devices, passed_along(): lax.ppermute(value, axis, [(source, source + steps) for source in range(f...  5.76 us
  transfers between devices with their start and end apart: 23, of which 18 were waited for; matrix products, arithmetic and copies ran while one was open for 3% of the time, Pallas kernels for 0%

commit v1 on v0

v1 whole, which is shorter than its diff:
```python
import functools

import jax
import jax.numpy as jnp
from jax import lax
from jax.experimental import pallas as pl
from jax.experimental.pallas import tpu as pltpu
from jax.sharding import PartitionSpec as P

GROUPS = 32
EPSILON = 1e-06
EDGE = 8
STATS = 8


def kernel(
    sections, tiles, height, width,
    frames_ref, cache_ref, weight_ref, bias_ref, gain_ref, offset_ref, out_ref,
    weight, main, outgoing, notes, drafts, old_notes, old_drafts, totals, wide, patches, state,
    weight_sem, main_sem, main_sent, note_sem, note_sent, first_sent, old_sem, old_sent,
):
    count, pixels, channels = frames_ref.shape
    context = cache_ref.shape[0]
    taps = weight_ref.shape[0] // (3 * channels * 3)
    halo = max(height, width)
    pitch = width + 2 * EDGE
    section = lax.axis_index("section")
    tile = lax.axis_index("tile")
    across = min(8, tiles // 2)
    down = tiles // across
    shift = across + 2

    def spot(index):
        image = lax.rem(index + shift, tiles)
        return image // across, lax.rem(image, across)

    row, column = spot(tile)

    def at_tile(peer_row, peer_column):
        return lax.rem(peer_row * across + peer_column + 2 * tiles - shift, tiles)

    def direction(peer):
        peer_row, peer_column = spot(peer)
        dy, dx = peer_row - row, peer_column - column
        near = (dy >= -1) & (dy <= 1) & (dx >= -1) & (dx <= 1)
        return jnp.where(near, (dy + 1) * 3 + dx + 1, 4)

    peers = [lax.rem(tile + step, tiles) for step in range(1, tiles)]
    last = section == sections - 1
    barrier = pltpu.get_barrier_semaphore()

    for peer in peers:
        pl.semaphore_signal(
            barrier, inc=1, device_id={"section": section, "tile": peer}, device_id_type=pl.DeviceIdType.MESH
        )

    @pl.when(section > 0)
    def _():
        for peer in peers + [tile]:
            pl.semaphore_signal(
                barrier, inc=1, device_id={"section": section - 1, "tile": peer},
                device_id_type=pl.DeviceIdType.MESH,
            )

    fetch = pltpu.make_async_copy(weight_ref, weight, weight_sem)
    fetch.start()

    def borders(target, values, stats):
        state[...] = values
        top, bottom = values[:width], values[pixels - width :]
        left = state[pl.ds(0, height, stride=width), :]
        right = state[pl.ds(width - 1, height, stride=width), :]
        pieces = [
            values[:width], top, values[:width],
            left, None, right,
            bottom, bottom, bottom,
        ]
        for place, piece in enumerate(pieces):
            if piece is not None:
                target[place, : piece.shape[0], :] = piece
            if stats is not None:
                target[place, halo : halo + STATS, :] = stats

    def measure_of(values):
        total = jnp.sum(values, axis=0, keepdims=True)
        squares = jnp.sum(values * values, axis=0, keepdims=True)
        line = lax.broadcasted_iota(jnp.int32, (STATS, channels), 0)
        return jnp.where(line == 0, total, jnp.where(line == 1, squares, 0.0))

    def post(source, frame, section_to, sent, peer):
        pltpu.make_async_remote_copy(
            src_ref=source.at[direction(peer)],
            dst_ref=notes.at[frame, tile],
            send_sem=sent.at[frame],
            recv_sem=note_sem.at[frame],
            device_id={"section": section_to, "tile": peer},
            device_id_type=pl.DeviceIdType.MESH,
        ).start()

    for frame in range(context):
        borders(old_drafts.at[frame], cache_ref[frame].astype(jnp.float32), None)

    @pl.when(section == 0)
    def _():
        for frame in range(count):
            values = frames_ref[frame].astype(jnp.float32)
            borders(drafts.at[count + frame], values, measure_of(values))

    pl.semaphore_wait(barrier, jnp.where(last, tiles - 1, 2 * tiles - 1))

    @pl.when(section == 0)
    def _():
        for frame in range(count):
            for peer in peers:
                post(drafts.at[count + frame], frame, 0, first_sent, peer)
            pltpu.make_async_copy(
                drafts.at[count + frame, 4], notes.at[frame, tile], note_sem.at[frame]
            ).start()

    for frame in range(context):
        for peer in peers:
            pltpu.make_async_remote_copy(
                src_ref=old_drafts.at[frame, direction(peer)],
                dst_ref=old_notes.at[frame, tile],
                send_sem=old_sent.at[frame],
                recv_sem=old_sem.at[frame],
                device_id={"section": section, "tile": peer},
                device_id_type=pl.DeviceIdType.MESH,
            ).start()

    around = {}
    for dy in (-1, 0, 1):
        for dx in (-1, 0, 1):
            if dy or dx:
                y, x = row + dy, column + dx
                inside = (y >= 0) & (y < down) & (x >= 0) & (x < across)
                around[dy, dx] = inside, jnp.where(inside, at_tile(y, x), peers[0])

    def lay_out(values, message, act):
        centre = act(values)

        def border(place, lines):
            inside, sender = around[place]
            piece = message(sender)[:lines]
            return jnp.where(inside, act(piece), 0.0)

        for y in range(height):
            wide[(1 + y) * pitch + EDGE : (1 + y) * pitch + EDGE + width, :] = centre[
                y * width : (y + 1) * width
            ]
        for dy, line in ((-1, 0), (1, height + 1)):
            base = line * pitch + EDGE
            wide[base : base + width, :] = border((dy, 0), width)
        for dx, spot_x in ((-1, EDGE - 1), (1, EDGE + width)):
            wide[pl.ds(pitch + spot_x, height, stride=pitch), :] = border((0, dx), height)
            for dy, line in ((-1, 0), (1, height + 1)):
                inside, sender = around[dy, dx]
                where_x = 0 if dx == 1 else width - 1
                piece = act(message(sender)[where_x : where_x + 1])
                wide[line * pitch + spot_x : line * pitch + spot_x + 1, :] = jnp.where(inside, piece, 0.0)
        for line in range(height + 2):
            for dx in range(3):
                start = line * pitch + EDGE - 1 + dx
                patches[line * width : (line + 1) * width, dx * channels : (dx + 1) * channels] = wide[
                    start : start + width, :
                ].astype(jnp.bfloat16)

    def convolved(*times):
        result = None
        for dy in range(3):
            kernels = [
                weight[(t * 3 + dy) * 3 * channels : (t * 3 + dy + 1) * 3 * channels, :] for t in times
            ]
            kernels = kernels[0] if len(kernels) == 1 else jnp.concatenate(kernels, axis=1)
            part = jnp.dot(
                patches[dy * width : dy * width + pixels, :], kernels, preferred_element_type=jnp.float32
            )
            result = part if result is None else result + part
        return result

    fetch.wait()
    fresh = set()

    def add(frame, value):
        if frame in fresh:
            totals[frame] += value
        else:
            totals[frame] = value
            fresh.add(frame)

    for old in range(context):
        pltpu.make_async_copy(
            old_notes.at[old, 0 : tiles - 1], old_notes.at[old, 0 : tiles - 1], old_sem.at[old]
        ).wait()
        lay_out(cache_ref[old].astype(jnp.float32), lambda sender: old_notes[old, sender], lambda v: v)
        reach = [t for t in range(taps) if 0 <= old - t < count]
        if reach:
            both = convolved(*reach)
            for at, t in enumerate(reach):
                add(old - t, both[:, at * channels : (at + 1) * channels])

    bias, gain, offset = bias_ref[...], gain_ref[...], offset_ref[...]
    members = pixels * tiles * (channels // GROUPS)
    lane = lax.broadcasted_iota(jnp.int32, (STATS, channels), 1)

    for frame in range(count):
        pltpu.make_async_copy(notes.at[frame], notes.at[frame], note_sem.at[frame]).wait()
        sums = notes[frame, 0, halo : halo + STATS]
        for sender in range(1, tiles):
            sums = sums + notes[frame, sender, halo : halo + STATS]
        step = 1
        while step < channels // GROUPS:
            sums = sums + jnp.where(
                (lane // step) % 2 == 0,
                pltpu.roll(sums, channels - step, 1),
                pltpu.roll(sums, step, 1),
            )
            step *= 2
        mean = sums[0:1] / members
        variance = jnp.maximum(sums[1:2] / members - mean * mean, 0.0)
        scale = gain / jnp.sqrt(variance + EPSILON)

        def act(values):
            value = (values - mean) * scale + offset
            return value / (1.0 + jnp.exp(-value))

        @pl.when(section > 0)
        def _():
            pltpu.make_async_copy(main.at[frame], main.at[frame], main_sem.at[frame]).wait()

        @pl.when(section == 0)
        def _():
            main[frame] = frames_ref[frame]

        values = main[frame].astype(jnp.float32)
        lay_out(values, lambda sender: notes[frame, sender], act)
        result = values + bias + convolved(taps - 1)
        if frame in fresh:
            result = result + totals[frame]
        rounded = result.astype(jnp.bfloat16)
        out_ref[frame] = rounded

        @pl.when(jnp.logical_not(last))
        def _():
            outgoing[frame] = rounded
            pltpu.make_async_remote_copy(
                src_ref=outgoing.at[frame],
                dst_ref=main.at[frame],
                send_sem=main_sent.at[frame],
                recv_sem=main_sem.at[frame],
                device_id={"section": section + 1, "tile": tile},
                device_id_type=pl.DeviceIdType.MESH,
            ).start()
            kept = rounded.astype(jnp.float32)
            borders(drafts.at[frame], kept, measure_of(kept))
            for peer in peers + [tile]:
                post(drafts.at[frame], frame, section + 1, note_sent, peer)

        reach = [t for t in range(taps - 1) if context + frame - t < count]
        if reach:
            both = convolved(*reach)
            for at, t in enumerate(reach):
                add(context + frame - t, both[:, at * channels : (at + 1) * channels])

    for frame in range(context):
        pltpu.make_async_copy(
            old_notes.at[frame, 0 : tiles - 1], old_notes.at[frame, 0 : tiles - 1], old_sent.at[frame]
        ).wait()

    for frame in range(count):
        @pl.when(section == 0)
        def _():
            pltpu.make_async_copy(
                notes.at[frame, 0 : tiles - 1], notes.at[frame, 0 : tiles - 1], first_sent.at[frame]
            ).wait()

        @pl.when(jnp.logical_not(last))
        def _():
            pltpu.make_async_copy(outgoing.at[frame], outgoing.at[frame], main_sent.at[frame]).wait()
            pltpu.make_async_copy(notes.at[frame], notes.at[frame], note_sent.at[frame]).wait()


def local(frames, cache, conv_weight, conv_bias, norm_gain, norm_bias):
    sections = lax.axis_size("section")
    tiles = lax.axis_size("tile")
    count, _, height, width, channels = frames.shape
    context = cache.shape[1]
    pixels = height * width
    lines = max(height, width)
    pitch = width + 2 * EDGE
    vmem = pl.BlockSpec(memory_space=pltpu.VMEM)
    dma = pltpu.SemaphoreType.DMA
    result = pl.pallas_call(
        functools.partial(kernel, sections, tiles, height, width),
        out_shape=jax.ShapeDtypeStruct((count, pixels, channels), jnp.bfloat16),
        in_specs=[vmem, vmem, pl.BlockSpec(memory_space=pl.ANY), vmem, vmem, vmem],
        out_specs=vmem,
        scratch_shapes=[
            pltpu.VMEM((27 * channels, channels), jnp.bfloat16),
            pltpu.VMEM((count, pixels, channels), jnp.bfloat16),
            pltpu.VMEM((count, pixels, channels), jnp.bfloat16),
            pltpu.VMEM((count, tiles, lines + STATS, channels), jnp.float32),
            pltpu.VMEM((2 * count, 9, lines + STATS, channels), jnp.float32),
            pltpu.VMEM((context, tiles, lines, channels), jnp.float32),
            pltpu.VMEM((context, 9, lines, channels), jnp.float32),
            pltpu.VMEM((count, pixels, channels), jnp.float32),
            pltpu.VMEM(((height + 2) * pitch, channels), jnp.float32),
            pltpu.VMEM(((height + 2) * width, 3 * channels), jnp.bfloat16),
            pltpu.VMEM((pixels, channels), jnp.float32),
            dma,
            dma((count,)),
            dma((count,)),
            dma((count,)),
            dma((count,)),
            dma((count,)),
            dma((context,)),
            dma((context,)),
        ],
        compiler_params=pltpu.CompilerParams(collective_id=0, has_side_effects=True),
    )(
        frames.reshape(count, pixels, channels),
        cache.reshape(context, pixels, channels),
        conv_weight.reshape(27 * channels, channels),
        conv_bias,
        norm_gain,
        norm_bias,
    )
    return result.reshape(1, count, 1, height, width, channels)


def solution(mesh):
    placed = (
        P("parts", "tile", None, None, None),
        P("section", "parts", "tile", None, None, None),
        P("section", None, None, None, None, None),
        P("section", None),
        P("section", None),
        P("section", None),
    )
    return jax.shard_map(
        local,
        mesh=mesh,
        in_specs=placed,
        out_specs=P("section", "parts", "tile", None, None, None),
        check_vma=False,
    )
```

time: 151 us -> 30.8 us (0.20)
  the two profiles are of different devices: /device:TPU:6 before, /device:TPU:3 now
where the time goes in v1:
time: 30.8 us; the launch traced here: 30.6 us
  Pallas kernels  28.9 us (94%)
  local copies, waits for them, and re-layouts  1.67 us (5%)
    pallas_call x1, Pallas kernels, local(): pl.pallas_call(functools.partial(kernel, sections, tiles, height, width),...  28.9 us
    unnamed x1, local copies, waits for them, and re-layouts  1.67 us

profile of v1, /device:TPU:3, one launch (start us, length us, event | category | flops | bytes accessed | tf_op | source)
XLA Modules:
  0.0 30.6 jit_solution(6285560370204187350)
XLA Ops:
  0.0 28.9 %shard_map.64 = bf16[4,256,128]{2,1,0:T(8,128)(2,1)} custom-call(bf16[4,256,128]{2,1,0:T(8,128)(2,1)} %bitcast.8, bf16[2,256,128]{2,1,0:T(8,128)(2,1)} %bitcast.9, bf16[3456,128]{1,0:T(8,128)(2,1)} %bitcast.7, f32[1,128]{1,0:T(1,128)} %bias_ref.1, f32[1,128]{1,0:T(1,128)} %gain_ref.1, f32[1,128]{1,0:T(1,128)} %offset_ref.1), custom_call_target="tpu_custom_call" | custom-call | tf_op jit(solution)/shard_map/pallas_call | solution.py:293
  29.0 1.7 %copy.9 = bf16[1,4,1,16,16,128]{5,4,3,2,1,0:T(8,128)(2,1)} copy(bf16[1,4,1,16,16,128]{5,4,3,2,1,0:T(8,128)(2,1)} %bitcast.6) | data formatting | bytes 524288

commit v2 on v1

v2 whole, which is shorter than its diff:
```python
import functools

import jax
import jax.numpy as jnp
from jax import lax
from jax.experimental import pallas as pl
from jax.experimental.pallas import tpu as pltpu
from jax.sharding import PartitionSpec as P

GROUPS = 32
EPSILON = 1e-06
EDGE = 8


SIDES = ((-1, 0), (0, -1), (0, 1), (1, 0))
CORNERS = ((-1, -1), (-1, 1), (1, -1), (1, 1))


def kernel(
    sections, tiles, height, width,
    frames_hbm, cache_hbm, weight_hbm, bias_ref, gain_ref, offset_ref, out_ref,
    weight, main, history, outgoing, notes, drafts, sides, columns,
    old_sides, old_columns, old_corners, old_drafts, totals, wide, patches, state,
    weight_sem, main_sem, main_sent, history_sem, note_sem, note_sent, first_sent,
    side_sem, side_sent, first_side_sent, old_sem, old_sent, corner_sem, corner_sent,
):
    count, pixels, channels = main.shape
    context = history.shape[0]
    taps = weight.shape[0] // (9 * channels)
    pitch = width + 2 * EDGE
    section = lax.axis_index("section")
    tile = lax.axis_index("tile")
    across = min(8, tiles // 2)
    down = tiles // across
    shift = across + 2
    mesh_id = pl.DeviceIdType.MESH
    first = section == 0
    onward = section < sections - 1
    image = lax.rem(tile + shift, tiles)
    row, column = image // across, lax.rem(image, across)
    peers = [lax.rem(tile + step, tiles) for step in range(1, tiles)]

    around = {}
    for dy, dx in SIDES + CORNERS:
        y, x = row + dy, column + dx
        inside = (y >= 0) & (y < down) & (x >= 0) & (x < across)
        there = lax.rem(y * across + x + 2 * tiles - shift, tiles)
        around[dy, dx] = inside, jnp.where(inside, there, peers[0])

    barrier = pltpu.get_barrier_semaphore()
    for peer in peers:
        pl.semaphore_signal(
            barrier, inc=1, device_id={"section": section, "tile": peer}, device_id_type=mesh_id
        )

    @pl.when(jnp.logical_not(first))
    def _():
        for peer in peers + [tile]:
            pl.semaphore_signal(
                barrier, inc=1, device_id={"section": section - 1, "tile": peer}, device_id_type=mesh_id
            )

    def fetch_frame(frame):
        return pltpu.make_async_copy(frames_hbm.at[frame], main.at[frame], main_sem.at[frame])

    fetch_weight = pltpu.make_async_copy(weight_hbm, weight, weight_sem)
    fetch_cache = [
        pltpu.make_async_copy(cache_hbm.at[old], history.at[old], history_sem.at[old])
        for old in range(context)
    ]

    @pl.when(first)
    def _():
        for frame in range(count):
            fetch_frame(frame).start()

    for fetch in fetch_cache:
        fetch.start()
    fetch_weight.start()

    def edge_columns(target, values):
        state[...] = values
        for at, x in enumerate((0, width - 1)):
            target[at] = state[pl.ds(x, height, stride=width), :].astype(jnp.bfloat16)

    def corner_of(values, dy, dx):
        at = (height - 1) * width * (dy == 1) + (width - 1) * (dx == 1)
        return values[at : at + 1]

    def write_notes(target, values):
        total = jnp.sum(values, axis=0, keepdims=True)
        squares = jnp.sum(values * values, axis=0, keepdims=True)
        for dy in (-1, 0, 1):
            for dx in (-1, 0, 1):
                place = (dy + 1) * 3 + dx + 1
                corner = corner_of(values, dy, dx)
                target[place] = jnp.concatenate([total, squares, corner, corner], axis=0)

    def post_notes(source, frame, section_to, sent, receivers):
        for peer in receivers:
            there = lax.rem(peer + shift, tiles)
            dy, dx = there // across - row, lax.rem(there, across) - column
            near = (dy >= -1) & (dy <= 1) & (dx >= -1) & (dx <= 1)
            pltpu.make_async_remote_copy(
                src_ref=source.at[jnp.where(near, (dy + 1) * 3 + dx + 1, 4)],
                dst_ref=notes.at[frame, tile],
                send_sem=sent.at[frame],
                recv_sem=note_sem.at[frame],
                device_id={"section": section_to, "tile": peer},
                device_id_type=mesh_id,
            ).start()

    def side_copies(rows, edges, landing, section_to, sent, received):
        copies = []
        for at, (dy, dx) in enumerate(SIDES):
            source = edges.at[int(dx == 1)]
            if dy:
                start = 0 if dy < 0 else pixels - width
                source = rows.at[start : start + width]
            inside, peer = around[dy, dx]
            copy = pltpu.make_async_remote_copy(
                src_ref=source,
                dst_ref=landing.at[3 - at],
                send_sem=sent.at[at],
                recv_sem=received.at[3 - at],
                device_id={"section": section_to, "tile": peer},
                device_id_type=mesh_id,
            )
            copies.append((inside, copy))
        return copies

    def each(copies, action):
        for inside, copy in copies:
            @pl.when(inside)
            def _():
                action(copy)

    def start(copy):
        copy.start()

    def departed(copy):
        copy.wait_send()

    def arrived(copies):
        for at, (_, copy) in enumerate(copies):
            inside, _ = copies[at // 4 * 4 + 3 - at % 4]

            @pl.when(inside)
            def _():
                copy.wait_recv()

    def old_copies(old):
        copies = side_copies(
            history.at[old], old_columns.at[old], old_sides.at[old], section, old_sent.at[old], old_sem.at[old]
        )
        for at, (dy, dx) in enumerate(CORNERS):
            inside, peer = around[dy, dx]
            copy = pltpu.make_async_remote_copy(
                src_ref=old_drafts.at[old, at],
                dst_ref=old_corners.at[old, 3 - at],
                send_sem=corner_sent.at[old, at],
                recv_sem=corner_sem.at[old, 3 - at],
                device_id={"section": section, "tile": peer},
                device_id_type=mesh_id,
            )
            copies.append((inside, copy))
        return copies

    def first_sides(frame):
        return side_copies(
            main.at[frame], columns.at[count + frame], sides.at[frame], section,
            first_side_sent.at[frame], side_sem.at[frame],
        )

    def next_sides(frame):
        return side_copies(
            outgoing.at[frame], columns.at[frame], sides.at[frame], section + onward.astype(jnp.int32),
            side_sent.at[frame], side_sem.at[frame],
        )

    def own_note(frame):
        return pltpu.make_async_copy(drafts.at[count + frame, 4], notes.at[frame, tile], note_sem.at[frame])

    def open_frame(frame):
        each(first_sides(frame), start)
        post_notes(drafts.at[count + frame], frame, section, first_sent, peers)
        own_note(frame).start()

    def prepare_frame(frame):
        fetch_frame(frame).wait()
        values = main[frame].astype(jnp.float32)
        edge_columns(columns.at[count + frame], values)
        write_notes(drafts.at[count + frame], values)

    @pl.when(first)
    def _():
        prepare_frame(0)

    pl.semaphore_wait(barrier, jnp.where(onward, 2 * tiles - 1, tiles - 1))

    @pl.when(first)
    def _():
        open_frame(0)

    for old in range(context):
        fetch_cache[old].wait()
        values = history[old].astype(jnp.float32)
        edge_columns(old_columns.at[old], values)
        for at, (dy, dx) in enumerate(CORNERS):
            old_drafts[old, at] = corner_of(values, dy, dx)
        each(old_copies(old), start)

    @pl.when(first)
    def _():
        for frame in range(1, count):
            prepare_frame(frame)
            open_frame(frame)

    def lay_out(values, side, corner, act):
        centre = act(values)
        for y in range(height):
            wide[(1 + y) * pitch + EDGE : (1 + y) * pitch + EDGE + width, :] = centre[
                y * width : (y + 1) * width
            ]
        for at, (dy, dx) in enumerate(SIDES):
            inside, _ = around[dy, dx]
            piece = jnp.where(inside, act(side(at).astype(jnp.float32)), 0.0)
            if dy:
                base = (0 if dy < 0 else height + 1) * pitch + EDGE
                wide[base : base + width, :] = piece
            else:
                base = pitch + (EDGE - 1 if dx < 0 else EDGE + width)
                wide[pl.ds(base, height, stride=pitch), :] = piece
        for at, (dy, dx) in enumerate(CORNERS):
            inside, sender = around[dy, dx]
            base = (0 if dy < 0 else height + 1) * pitch + (EDGE - 1 if dx < 0 else EDGE + width)
            wide[base : base + 1, :] = jnp.where(inside, act(corner(at, sender)), 0.0)
        for line in range(height + 2):
            for dx in range(3):
                at = line * pitch + EDGE - 1 + dx
                patches[line * width : (line + 1) * width, dx * channels : (dx + 1) * channels] = wide[
                    at : at + width, :
                ].astype(jnp.bfloat16)

    def convolved(*times):
        result = None
        for dy in range(3):
            kernels = [
                weight[(t * 3 + dy) * 3 * channels : (t * 3 + dy + 1) * 3 * channels, :] for t in times
            ]
            kernels = kernels[0] if len(kernels) == 1 else jnp.concatenate(kernels, axis=1)
            part = jnp.dot(
                patches[dy * width : dy * width + pixels, :], kernels, preferred_element_type=jnp.float32
            )
            result = part if result is None else result + part
        return result

    fetch_weight.wait()
    fresh = set()

    def spread(newest, times):
        reach = [t for t in times if 0 <= newest - t < count]
        if reach:
            both = convolved(*reach)
        for at, t in enumerate(reach):
            value = both[:, at * channels : (at + 1) * channels]
            if newest - t in fresh:
                totals[newest - t] += value
            else:
                totals[newest - t] = value
                fresh.add(newest - t)

    for old in range(context):
        arrived(old_copies(old))
        lay_out(
            history[old].astype(jnp.float32),
            lambda at: old_sides[old, at],
            lambda at, sender: old_corners[old, at],
            lambda values: values,
        )
        spread(old, range(taps))

    bias, gain, offset = bias_ref[...], gain_ref[...], offset_ref[...]
    members = pixels * tiles * (channels // GROUPS)
    lane = lax.broadcasted_iota(jnp.int32, (2, channels), 1)

    for frame in range(count):
        pltpu.make_async_copy(notes.at[frame], notes.at[frame], note_sem.at[frame]).wait()
        arrived(next_sides(frame))

        @pl.when(jnp.logical_not(first))
        def _():
            fetch_frame(frame).wait()

        sums = notes[frame, 0, 0:2]
        for sender in range(1, tiles):
            sums = sums + notes[frame, sender, 0:2]
        step = 1
        while step < channels // GROUPS:
            sums = sums + jnp.where(
                (lane // step) % 2 == 0,
                jnp.roll(sums, channels - step, 1),
                jnp.roll(sums, step, 1),
            )
            step *= 2
        mean = sums[0:1] / members
        variance = jnp.maximum(sums[1:2] / members - mean * mean, 0.0)
        scale = gain / jnp.sqrt(variance + EPSILON)

        def act(values):
            value = (values - mean) * scale + offset
            return value / (1.0 + jnp.exp(-value))

        values = main[frame].astype(jnp.float32)
        lay_out(
            values, lambda at: sides[frame, at], lambda at, sender: notes[frame, sender, 2:3], act
        )
        result = values + bias + convolved(taps - 1)
        if frame in fresh:
            result = result + totals[frame]
        rounded = result.astype(jnp.bfloat16)
        out_ref[frame] = rounded

        @pl.when(onward)
        def _():
            outgoing[frame] = rounded
            pltpu.make_async_remote_copy(
                src_ref=outgoing.at[frame],
                dst_ref=main.at[frame],
                send_sem=main_sent.at[frame],
                recv_sem=main_sem.at[frame],
                device_id={"section": section + 1, "tile": tile},
                device_id_type=mesh_id,
            ).start()
            kept = rounded.astype(jnp.float32)
            write_notes(drafts.at[frame], kept)
            post_notes(drafts.at[frame], frame, section + 1, note_sent, peers + [tile])
            edge_columns(columns.at[frame], kept)
            each(next_sides(frame), start)

        spread(context + frame, range(taps - 1))

    for old in range(context):
        each(old_copies(old), departed)

    @pl.when(first)
    def _():
        for frame in range(count):
            each(first_sides(frame), departed)
            some = notes.at[frame, 0 : tiles - 1]
            pltpu.make_async_copy(some, some, first_sent.at[frame]).wait()

    @pl.when(onward)
    def _():
        for frame in range(count):
            pltpu.make_async_copy(outgoing.at[frame], outgoing.at[frame], main_sent.at[frame]).wait()
            pltpu.make_async_copy(notes.at[frame], notes.at[frame], note_sent.at[frame]).wait()
            each(next_sides(frame), departed)


def local(frames, cache, conv_weight, conv_bias, norm_gain, norm_bias):
    sections = lax.axis_size("section")
    tiles = lax.axis_size("tile")
    count, _, height, width, channels = frames.shape
    context = cache.shape[1]
    pixels = height * width
    pitch = width + 2 * EDGE
    rows = conv_weight.size // channels
    vmem = pl.BlockSpec(memory_space=pltpu.VMEM)
    anywhere = pl.BlockSpec(memory_space=pl.ANY)
    dma = pltpu.SemaphoreType.DMA
    half, full = jnp.bfloat16, jnp.float32
    result = pl.pallas_call(
        functools.partial(kernel, sections, tiles, height, width),
        out_shape=pltpu.VMEM((count, pixels, channels), jnp.bfloat16),
        in_specs=[anywhere, anywhere, anywhere, vmem, vmem, vmem],
        out_specs=vmem,
        scratch_shapes=[
            pltpu.VMEM((rows, channels), half),
            pltpu.VMEM((count, pixels, channels), half),
            pltpu.VMEM((context, pixels, channels), half),
            pltpu.VMEM((count, pixels, channels), half),
            pltpu.VMEM((count, tiles, 4, channels), full),
            pltpu.VMEM((2 * count, 9, 4, channels), full),
            pltpu.VMEM((count, 4, width, channels), half),
            pltpu.VMEM((2 * count, 2, height, channels), half),
            pltpu.VMEM((context, 4, width, channels), half),
            pltpu.VMEM((context, 2, height, channels), half),
            pltpu.VMEM((context, 4, 1, channels), full),
            pltpu.VMEM((context, 4, 1, channels), full),
            pltpu.VMEM((count, pixels, channels), full),
            pltpu.VMEM(((height + 2) * pitch, channels), full),
            pltpu.VMEM(((height + 2) * width, 3 * channels), half),
            pltpu.VMEM((pixels, channels), full),
            dma,
            dma((count,)),
            dma((count,)),
            dma((context,)),
            dma((count,)),
            dma((count,)),
            dma((count,)),
            dma((count, 4)),
            dma((count, 4)),
            dma((count, 4)),
            dma((context, 4)),
            dma((context, 4)),
            dma((context, 4)),
            dma((context, 4)),
        ],
        compiler_params=pltpu.CompilerParams(collective_id=0, has_side_effects=True),
    )(
        frames.reshape(count, pixels, channels),
        cache.reshape(context, pixels, channels),
        conv_weight.reshape(rows, channels),
        conv_bias,
        norm_gain,
        norm_bias,
    )
    return result.reshape(1, count, 1, height, width, channels)


def solution(mesh):
    placed = (
        P("parts", "tile", None, None, None),
        P("section", "parts", "tile", None, None, None),
        P("section", None, None, None, None, None),
        P("section", None),
        P("section", None),
        P("section", None),
    )
    return jax.shard_map(
        local,
        mesh=mesh,
        in_specs=placed,
        out_specs=P("section", "parts", "tile", None, None, None),
        check_vma=False,
    )
```

time: 30.8 us -> 26.6 us (0.86)
  Pallas kernels: 28.9 us -> 25.8 us
  local copies, waits for them, and re-layouts: 1.67 us -> 0.71 us
    pallas_call x1, Pallas kernels: 28.9 us -> 25.8 us  [local(): pl.pallas_call(functools.partial(kernel, sections, tiles, height, width),...]
    unnamed x1, local copies, waits for them, and re-layouts: 1.67 us -> 0.71 us
where the time goes in v2:
time: 26.6 us; the launch traced here: 26.5 us
  Pallas kernels  25.8 us (97%)
  local copies, waits for them, and re-layouts  0.71 us (3%)
    pallas_call x1, Pallas kernels, local(): pl.pallas_call(functools.partial(kernel, sections, tiles, height, width),...  25.8 us
    unnamed x1, local copies, waits for them, and re-layouts  0.71 us

profile of v2, /device:TPU:3, one launch (start us, length us, event | category | flops | bytes accessed | tf_op | source)
XLA Modules:
  0.0 26.5 jit_solution(2779676212130273159)
XLA Ops:
  0.0 25.8 %shard_map.64 = bf16[4,256,128]{2,1,0:T(8,128)(2,1)S(1)} custom-call(bf16[4,256,128]{2,1,0:T(8,128)(2,1)} %bitcast.8, bf16[2,256,128]{2,1,0:T(8,128)(2,1)} %bitcast.9, bf16[3456,128]{1,0:T(8,128)(2,1)} %bitcast.7, f32[1,128]{1,0:T(1,128)} %bias_ref.1, f32[1,128]{1,0:T(1,128)} %gain_ref.1, f32[1,128]{1,0:T(1,128)} %offset_ref.1), custom_call_target="tpu_custom_call" | custom-call | tf_op jit(solution)/shard_map/pallas_call | solution.py:373
  25.8 0.7 %copy.9 = bf16[1,4,1,16,16,128]{5,4,3,2,1,0:T(8,128)(2,1)} copy(bf16[1,4,1,16,16,128]{5,4,3,2,1,0:T(8,128)(2,1)S(1)} %bitcast.6) | data formatting | bytes 524288

commit v3 on v2

--- a/solution.py
+++ b/solution.py
@@ -18,10 +18,10 @@
 
 def kernel(
     sections, tiles, height, width,
-    frames_hbm, cache_hbm, weight_hbm, bias_ref, gain_ref, offset_ref, out_ref,
-    weight, main, history, outgoing, notes, drafts, sides, columns,
+    frames_hbm, cache_hbm, weight_hbm, bias_hbm, gain_hbm, offset_hbm, out_ref,
+    weight, vectors, main, history, outgoing, notes, drafts, sides, columns,
     old_sides, old_columns, old_corners, old_drafts, totals, wide, patches, state,
-    weight_sem, main_sem, main_sent, history_sem, note_sem, note_sent, first_sent,
+    weight_sem, vector_sem, main_sem, main_sent, history_sem, note_sem, note_sent, first_sent,
     side_sem, side_sent, first_side_sent, old_sem, old_sent, corner_sem, corner_sent,
 ):
     count, pixels, channels = main.shape
@@ -74,9 +74,12 @@
         for frame in range(count):
             fetch_frame(frame).start()
 
-    for fetch in fetch_cache:
+    fetch_vectors = [
+        pltpu.make_async_copy(source, vectors.at[at], vector_sem.at[at])
+        for at, source in enumerate((bias_hbm, gain_hbm, offset_hbm))
+    ]
+    for fetch in fetch_cache + [fetch_weight] + fetch_vectors:
         fetch.start()
-    fetch_weight.start()
 
     def edge_columns(target, values):
         state[...] = values
@@ -243,17 +246,13 @@
                 ].astype(jnp.bfloat16)
 
     def convolved(*times):
-        result = None
-        for dy in range(3):
-            kernels = [
-                weight[(t * 3 + dy) * 3 * channels : (t * 3 + dy + 1) * 3 * channels, :] for t in times
-            ]
-            kernels = kernels[0] if len(kernels) == 1 else jnp.concatenate(kernels, axis=1)
-            part = jnp.dot(
-                patches[dy * width : dy * width + pixels, :], kernels, preferred_element_type=jnp.float32
-            )
-            result = part if result is None else result + part
-        return result
+        rows = jnp.concatenate(
+            [patches[dy * width : dy * width + pixels, :] for dy in range(3)], axis=1
+        )
+        depth = 9 * channels
+        kernels = [weight[t * depth : (t + 1) * depth, :] for t in times]
+        kernels = kernels[0] if len(kernels) == 1 else jnp.concatenate(kernels, axis=1)
+        return jnp.dot(rows, kernels, preferred_element_type=jnp.float32)
 
     fetch_weight.wait()
     fresh = set()
@@ -280,7 +279,9 @@
         )
         spread(old, range(taps))
 
-    bias, gain, offset = bias_ref[...], gain_ref[...], offset_ref[...]
+    for fetch in fetch_vectors:
+        fetch.wait()
+    bias, gain, offset = vectors[0], vectors[1], vectors[2]
     members = pixels * tiles * (channels // GROUPS)
     lane = lax.broadcasted_iota(jnp.int32, (2, channels), 1)
 
@@ -324,6 +325,11 @@
         @pl.when(onward)
         def _():
             outgoing[frame] = rounded
+            kept = rounded.astype(jnp.float32)
+            write_notes(drafts.at[frame], kept)
+            post_notes(drafts.at[frame], frame, section + 1, note_sent, peers + [tile])
+            edge_columns(columns.at[frame], kept)
+            each(next_sides(frame), start)
             pltpu.make_async_remote_copy(
                 src_ref=outgoing.at[frame],
                 dst_ref=main.at[frame],
@@ -332,11 +338,6 @@
                 device_id={"section": section + 1, "tile": tile},
                 device_id_type=mesh_id,
             ).start()
-            kept = rounded.astype(jnp.float32)
-            write_notes(drafts.at[frame], kept)
-            post_notes(drafts.at[frame], frame, section + 1, note_sent, peers + [tile])
-            edge_columns(columns.at[frame], kept)
-            each(next_sides(frame), start)
 
         spread(context + frame, range(taps - 1))
 
@@ -373,10 +374,11 @@
     result = pl.pallas_call(
         functools.partial(kernel, sections, tiles, height, width),
         out_shape=pltpu.VMEM((count, pixels, channels), jnp.bfloat16),
-        in_specs=[anywhere, anywhere, anywhere, vmem, vmem, vmem],
+        in_specs=[anywhere] * 6,
         out_specs=vmem,
         scratch_shapes=[
             pltpu.VMEM((rows, channels), half),
+            pltpu.VMEM((3, 1, channels), full),
             pltpu.VMEM((count, pixels, channels), half),
             pltpu.VMEM((context, pixels, channels), half),
             pltpu.VMEM((count, pixels, channels), half),
@@ -393,6 +395,7 @@
             pltpu.VMEM(((height + 2) * width, 3 * channels), half),
             pltpu.VMEM((pixels, channels), full),
             dma,
+            dma((3,)),
             dma((count,)),
             dma((count,)),
             dma((context,)),

time: 26.6 us -> 25.7 us (0.966)
  Pallas kernels: 25.8 us -> 24.8 us
    pallas_call x1, Pallas kernels: 25.8 us -> 24.8 us  [local(): pl.pallas_call(functools.partial(kernel, sections, tiles, height, width),...]
where the time goes in v3:
time: 25.7 us; the launch traced here: 25.6 us
  Pallas kernels  24.8 us (96%)
  local copies, waits for them, and re-layouts  0.71 us (3%)
    pallas_call x1, Pallas kernels, local(): pl.pallas_call(functools.partial(kernel, sections, tiles, height, width),...  24.8 us
    unnamed x1, local copies, waits for them, and re-layouts  0.71 us

profile of v3, /device:TPU:3, one launch (start us, length us, event | category | flops | bytes accessed | tf_op | source)
XLA Modules:
  0.0 25.6 jit_solution(11374397115385943878)
XLA Ops:
  0.0 24.8 %shard_map.64 = bf16[4,256,128]{2,1,0:T(8,128)(2,1)S(1)} custom-call(bf16[4,256,128]{2,1,0:T(8,128)(2,1)} %bitcast.8, bf16[2,256,128]{2,1,0:T(8,128)(2,1)} %bitcast.9, bf16[3456,128]{1,0:T(8,128)(2,1)} %bitcast.7, f32[1,128]{1,0:T(1,128)} %bias_hbm.1, f32[1,128]{1,0:T(1,128)} %gain_hbm.1, f32[1,128]{1,0:T(1,128)} %offset_hbm.1), custom_call_target="tpu_custom_call" | custom-call | tf_op jit(solution)/shard_map/pallas_call | solution.py:374
  24.8 0.7 %copy.9 = bf16[1,4,1,16,16,128]{5,4,3,2,1,0:T(8,128)(2,1)} copy(bf16[1,4,1,16,16,128]{5,4,3,2,1,0:T(8,128)(2,1)S(1)} %bitcast.6) | data formatting | bytes 524288

commit v4 on v3

--- a/solution.py
+++ b/solution.py
@@ -107,7 +107,7 @@
             pltpu.make_async_remote_copy(
                 src_ref=source.at[jnp.where(near, (dy + 1) * 3 + dx + 1, 4)],
                 dst_ref=notes.at[frame, tile],
-                send_sem=sent.at[frame],
+                send_sem=sent,
                 recv_sem=note_sem.at[frame],
                 device_id={"section": section_to, "tile": peer},
                 device_id_type=mesh_id,
@@ -141,9 +141,6 @@
     def start(copy):
         copy.start()
 
-    def departed(copy):
-        copy.wait_send()
-
     def arrived(copies):
         for at, (_, copy) in enumerate(copies):
             inside, _ = copies[at // 4 * 4 + 3 - at % 4]
@@ -154,14 +151,14 @@
 
     def old_copies(old):
         copies = side_copies(
-            history.at[old], old_columns.at[old], old_sides.at[old], section, old_sent.at[old], old_sem.at[old]
+            history.at[old], old_columns.at[old], old_sides.at[old], section, old_sent, old_sem.at[old]
         )
         for at, (dy, dx) in enumerate(CORNERS):
             inside, peer = around[dy, dx]
             copy = pltpu.make_async_remote_copy(
                 src_ref=old_drafts.at[old, at],
                 dst_ref=old_corners.at[old, 3 - at],
-                send_sem=corner_sent.at[old, at],
+                send_sem=corner_sent.at[at],
                 recv_sem=corner_sem.at[old, 3 - at],
                 device_id={"section": section, "tile": peer},
                 device_id_type=mesh_id,
@@ -172,13 +169,13 @@
     def first_sides(frame):
         return side_copies(
             main.at[frame], columns.at[count + frame], sides.at[frame], section,
-            first_side_sent.at[frame], side_sem.at[frame],
+            first_side_sent, side_sem.at[frame],
         )
 
     def next_sides(frame):
         return side_copies(
             outgoing.at[frame], columns.at[frame], sides.at[frame], section + onward.astype(jnp.int32),
-            side_sent.at[frame], side_sem.at[frame],
+            side_sent, side_sem.at[frame],
         )
 
     def own_note(frame):
@@ -333,7 +330,7 @@
             pltpu.make_async_remote_copy(
                 src_ref=outgoing.at[frame],
                 dst_ref=main.at[frame],
-                send_sem=main_sent.at[frame],
+                send_sem=main_sent,
                 recv_sem=main_sem.at[frame],
                 device_id={"section": section + 1, "tile": tile},
                 device_id_type=mesh_id,
@@ -341,22 +338,30 @@
 
         spread(context + frame, range(taps - 1))
 
-    for old in range(context):
-        each(old_copies(old), departed)
+    def departed(buffer, sent):
+        pltpu.make_async_copy(buffer, buffer, sent).wait()
+
+    def sides_departed(buffer, sent, places):
+        for at, place in enumerate(places):
+            inside, _ = around[place]
+
+            @pl.when(inside)
+            def _():
+                departed(buffer.at[:, at], sent.at[at])
+
+    sides_departed(old_sides, old_sent, SIDES)
+    sides_departed(old_corners, corner_sent, CORNERS)
 
     @pl.when(first)
     def _():
-        for frame in range(count):
-            each(first_sides(frame), departed)
-            some = notes.at[frame, 0 : tiles - 1]
-            pltpu.make_async_copy(some, some, first_sent.at[frame]).wait()
+        departed(notes.at[:, 0 : tiles - 1], first_sent)
+        sides_departed(sides, first_side_sent, SIDES)
 
     @pl.when(onward)
     def _():
-        for frame in range(count):
-            pltpu.make_async_copy(outgoing.at[frame], outgoing.at[frame], main_sent.at[frame]).wait()
-            pltpu.make_async_copy(notes.at[frame], notes.at[frame], note_sent.at[frame]).wait()
-            each(next_sides(frame), departed)
+        departed(outgoing, main_sent)
+        departed(notes, note_sent)
+        sides_departed(sides, side_sent, SIDES)
 
 
 def local(frames, cache, conv_weight, conv_bias, norm_gain, norm_bias):
@@ -397,18 +402,18 @@
             dma,
             dma((3,)),
             dma((count,)),
-            dma((count,)),
+            dma,
             dma((context,)),
             dma((count,)),
-            dma((count,)),
-            dma((count,)),
+            dma,
+            dma,
             dma((count, 4)),
-            dma((count, 4)),
-            dma((count, 4)),
+            dma((4,)),
+            dma((4,)),
             dma((context, 4)),
+            dma((4,)),
             dma((context, 4)),
-            dma((context, 4)),
-            dma((context, 4)),
+            dma((4,)),
         ],
         compiler_params=pltpu.CompilerParams(collective_id=0, has_side_effects=True),
     )(

time: 25.7 us -> 25.3 us (0.984)
  Pallas kernels: 24.8 us -> 24.4 us
    pallas_call x1, Pallas kernels: 24.8 us -> 24.4 us  [local(): pl.pallas_call(functools.partial(kernel, sections, tiles, height, width),...]
where the time goes in v4:
time: 25.3 us; the launch traced here: 25.1 us
  Pallas kernels  24.4 us (96%)
  local copies, waits for them, and re-layouts  0.71 us (3%)
    pallas_call x1, Pallas kernels, local(): pl.pallas_call(functools.partial(kernel, sections, tiles, height, width),...  24.4 us
    unnamed x1, local copies, waits for them, and re-layouts  0.71 us

profile of v4, /device:TPU:3, one launch (start us, length us, event | category | flops | bytes accessed | tf_op | source)
XLA Modules:
  0.0 25.1 jit_solution(18008612560552593613)
XLA Ops:
  0.0 24.4 %shard_map.64 = bf16[4,256,128]{2,1,0:T(8,128)(2,1)S(1)} custom-call(bf16[4,256,128]{2,1,0:T(8,128)(2,1)} %bitcast.8, bf16[2,256,128]{2,1,0:T(8,128)(2,1)} %bitcast.9, bf16[3456,128]{1,0:T(8,128)(2,1)} %bitcast.7, f32[1,128]{1,0:T(1,128)} %bias_hbm.1, f32[1,128]{1,0:T(1,128)} %gain_hbm.1, f32[1,128]{1,0:T(1,128)} %offset_hbm.1), custom_call_target="tpu_custom_call" | custom-call | tf_op jit(solution)/shard_map/pallas_call | solution.py:379
  24.4 0.7 %copy.9 = bf16[1,4,1,16,16,128]{5,4,3,2,1,0:T(8,128)(2,1)} copy(bf16[1,4,1,16,16,128]{5,4,3,2,1,0:T(8,128)(2,1)S(1)} %bitcast.6) | data formatting | bytes 524288
